TPU v7x, 32 devices: a whole 2x2x4 slice. The times are simulated.
32 devices in a mesh: ma: 2 (over y), an: 4 (over z), ka: 4 (over x, core).
Axes of the slice: x: 2, y: 2, z: 4, core: 2. Of those that a mesh axis runs over, the one named last changes fastest.
Arguments:
- left_matrix: float32 [16384, 2048], P(('ka', 'an'), 'ma'), may hold values from -6 to 6
- right_matrix: float32 [16384, 3072], P(('ka', 'ma'), 'an'), may hold values from -0.046875 to 0.046875
Outputs:
- product: float32 [2048, 3072], P(('ma', 'ka'), 'an')
All inputs are finite; a program needn't handle non-finite values.
Results may differ from a plain program's by a relative error of at most 0.000098.
Values sent between devices are 32-bit elements; how exact they have to be, the bound alone decides.
A program may use at most 128 MiB of HBM per device.

v0:
```python
import jax
import jax.numpy as jnp
from jax import lax
from jax.sharding import PartitionSpec as P


def multiply(left_part, right_part):
    return lax.dot_general(
        left_part,
        right_part,
        (((0,), (0,)), ((), ())),
        precision=lax.Precision.HIGHEST,
        preferred_element_type=jnp.float32,
    )


def per_device(left_matrix, right_matrix):
    b_block = lax.all_gather(right_matrix, "ma", axis=0, tiled=True)
    a_block = lax.all_gather(left_matrix, "an", axis=0, tiled=True)
    partial_value = multiply(a_block, b_block)
    summed = lax.psum_scatter(partial_value, "ka", scatter_dimension=0, tiled=True)
    return summed


def solution(mesh):
    placed = (P(("ka", "an"), "ma"), P(("ka", "ma"), "an"))
    return jax.shard_map(
        per_device, mesh=mesh, in_specs=placed, out_specs=P(("ma", "ka"), "an"), check_vma=False
    )
```

profile of v0, /device:TPU:0, one launch (start us, length us, event | category | flops | bytes accessed | tf_op | source)
XLA Modules:
  0.0 542.0 jit_solution(16185840921908149508)
XLA Ops:
  6.5 0.0 all-gather.5.cloned.1.call-start
  6.5 0.7 all-gather.5.cloned.1.call-update
  7.3 0.0 all-gather.3.cloned.1.call-start
  7.3 0.7 all-gather.3.cloned.1.call-update
  8.0 0.0 reduce-scatter.2.cloned.1.call-start
  8.1 156.1 %all-gather.5.cloned.1.call-done = f32[4096,768]{1,0:T(8,128)} async-done(((f32[2048,768]{1,0:T(8,128)}), f32[4096,768]{1,0:T(8,128)}) %all-gather.5.cloned.1.call-update) | async-done | bytes 12582928 | tf_op jit(solution)/shard_map/all_gather | solution.py:18
  164.1 288.4 %all-gather.3.cloned.1.call-done = f32[4096,1024]{1,0:T(8,128)} async-done(((f32[1024,1024]{1,0:T(8,128)}), f32[4096,1024]{1,0:T(8,128)}) %all-gather.3.cloned.1.call-update) | async-done | bytes 16777232 | tf_op jit(solution)/shard_map/all_gather | solution.py:19
  452.5 46.7 %fusion = f32[1024,768]{1,0:T(8,128)} fusion(f32[4096,1024]{1,0:T(8,128)} %all-gather.3.cloned.1.call-done, f32[4096,768]{1,0:T(8,128)} %all-gather.5.cloned.1.call-done), kind=kOutput, calls=%fused_computation | convolution fusion | flops 38654705664 | bytes 32505856 | tf_op jit(solution)/shard_map/dot_general | solution.py:8
  499.2 0.0 reduce-scatter.2.cloned.1.call-update
  499.3 36.2 %reduce-scatter.2.cloned.1.call-done = f32[256,768]{1,0:T(8,128)} async-done(((f32[1024,768]{1,0:T(8,128)}), f32[256,768]{1,0:T(8,128)}) %reduce-scatter.2.cloned.1.call-update) | async-done | bytes 786448 | tf_op jit(solution)/shard_map/reduce_scatter | solution.py:21
Async XLA Ops:
  6.5 157.6 %all-gather.5.cloned.1.call-start = ((), (), s32[]{:S(2)}) async-start(), calls=%async_computation.2 | async-start | bytes 18874368 | tf_op jit(solution)/shard_map/all_gather | solution.py:18
  7.3 445.2 %all-gather.3.cloned.1.call-start = ((), (), s32[]{:S(2)}) async-start(), calls=%async_computation.1 | async-start | bytes 20971520 | tf_op jit(solution)/shard_map/all_gather | solution.py:19
  8.0 527.5 %reduce-scatter.2.cloned.1.call-start = ((), (), s32[]{:S(2)}) async-start(), calls=%async_computation.3 | async-start | bytes 3932160 | tf_op jit(solution)/shard_map/reduce_scatter | solution.py:21
Sparse Core Ops, SparseCore 0:
  8.9 155.2 all-gather.4
  165.7 286.7 all-gather.2
  499.4 36.0 reduce-scatter.1
where the time goes:
time: 542 us
  waiting for transfers between devices  482 us (89%)
  matrix products  46.7 us (9%)
  between operations  13.1 us (2%)
    all_gather x1, waiting for transfers between devices, per_device(): a_block = lax.all_gather(left_matrix, 'an', axis=0, tiled=True)  288 us
    all_gather x1, waiting for transfers between devices, per_device(): b_block = lax.all_gather(right_matrix, 'ma', axis=0, tiled=True)  156 us
    dot_general x1, matrix products, multiply(): lax.dot_general(left_part, right_part, (((0,), (0,)), ((), ())), precisio...  46.7 us
    reduce_scatter x1, waiting for transfers between devices, per_device(): lax.psum_scatter(partial_value, 'ka', scatter_dimension=0, tiled=True)  36.2 us
  transfers between devices with their start and end apart: 3, of which 3 were waited for; matrix products, arithmetic and copies ran while one was open for 0% of the time, Pallas kernels for 0%

commit v1 on v0

--- a/solution.py
+++ b/solution.py
@@ -16,7 +16,12 @@
 
 def per_device(left_matrix, right_matrix):
     b_block = lax.all_gather(right_matrix, "ma", axis=0, tiled=True)
-    a_block = lax.all_gather(left_matrix, "an", axis=0, tiled=True)
+    ring = [left_matrix]
+    for hop in range(3):
+        ring.append(lax.ppermute(ring[-1], "an", [(dev, (dev + 1) % 4) for dev in range(4)]))
+    a_block = jnp.roll(
+        jnp.concatenate(ring[::-1], axis=0), (lax.axis_index("an") + 1) * ring[0].shape[0], axis=0
+    )
     partial_value = multiply(a_block, b_block)
     summed = lax.psum_scatter(partial_value, "ka", scatter_dimension=0, tiled=True)
     return summed

time: 542 us -> 414 us (0.76)
  waiting for transfers between devices: 482 us -> 316 us
  local copies, waits for them, and re-layouts: 0 us -> 35.4 us
    all_gather x1 -> x0, waiting for transfers between devices: 288 us -> none  [per_device(): a_block = lax.all_gather(left_matrix, 'an', axis=0, tiled=True)]
    ppermute x0 -> x3, waiting for transfers between devices: none -> 280 us  [per_device(): lax.ppermute(ring[-1], 'an', [(dev, (dev + 1) % 4) for dev in range(4)])]
    all_gather x1, waiting for transfers between devices: 156 us -> 0.01 us  [per_device(): b_block = lax.all_gather(right_matrix, 'ma', axis=0, tiled=True)]
    unnamed x0 -> x9, local copies, waits for them, and re-layouts: none -> 33.1 us
  transfers between devices with their start and end apart: 3 -> 5, of which waited for: 3 -> 4; matrix products, arithmetic and copies ran while one was open for 0% -> 9% of each run, Pallas kernels for 0% -> 0%
where the time goes in v1:
time: 414 us
  waiting for transfers between devices  316 us (76%)
  matrix products  46.7 us (11%)
  local copies, waits for them, and re-layouts  35.4 us (9%)
  between operations  13.4 us (3%)
    ppermute x3, waiting for transfers between devices, per_device(): lax.ppermute(ring[-1], 'an', [(dev, (dev + 1) % 4) for dev in range(4)])  280 us
    dot_general x1, matrix products, multiply(): lax.dot_general(left_part, right_part, (((0,), (0,)), ((), ())), precisio...  46.7 us
    reduce_scatter x1, waiting for transfers between devices, per_device(): lax.psum_scatter(partial_value, 'ka', scatter_dimension=0, tiled=True)  35.8 us
    unnamed x9, local copies, waits for them, and re-layouts  33.1 us
  transfers between devices with their start and end apart: 5, of which 4 were waited for; matrix products, arithmetic and copies ran while one was open for 9% of the time, Pallas kernels for 0%

profile of v1, /device:TPU:0, one launch (start us, length us, event | category | flops | bytes accessed | tf_op | source)
XLA Modules:
  0.0 414.1 jit_solution(17562172633027988802)
XLA Ops:
  6.5 0.0 all-gather.2.cloned.1.call-start
  6.5 3.1 collective-permute-start
  9.6 0.0 all-gather.2.cloned.1.call-update
  9.6 0.0 reduce-scatter.2.cloned.1.call-start
  9.7 92.8 %collective-permute-done = f32[1024,1024]{1,0:T(8,128)} collective-permute-done((f32[1024,1024]{1,0:T(8,128)}, f32[1024,1024]{1,0:T(8,128)}, u32[]{:S(2)}, u32[]{:S(2)}) %collective-permute-start) | collective-permute-done | bytes 4194336 | tf_op jit(solution)/shard_map/ppermute | solution.py:21
  102.5 0.0 collective-permute-start.1
  102.5 93.8 %collective-permute-done.1 = f32[1024,1024]{1,0:T(8,128)} collective-permute-done((f32[1024,1024]{1,0:T(8,128)}, f32[1024,1024]{1,0:T(8,128)}, u32[]{:S(2)}, u32[]{:S(2)}) %collective-permute-start.1) | collective-permute-done | bytes 4194336 | tf_op jit(solution)/shard_map/ppermute | solution.py:21
  196.3 0.0 collective-permute-start.2
  196.4 0.0 copy-start
  196.4 93.0 %collective-permute-done.2 = f32[1024,1024]{1,0:T(8,128)} collective-permute-done((f32[1024,1024]{1,0:T(8,128)}, f32[1024,1024]{1,0:T(8,128)}, u32[]{:S(2)}, u32[]{:S(2)}) %collective-permute-start.2) | collective-permute-done | bytes 4194336 | tf_op jit(solution)/shard_map/ppermute | solution.py:21
  289.3 4.7 %constant_dynamic-update-slice_fusion.7 = f32[8192,1024]{1,0:T(8,128)} fusion(f32[1024,1024]{1,0:T(8,128)} %collective-permute-done.2), kind=kLoop, calls=%fused_computation.9 | loop fusion | bytes 8388608
  294.1 4.8 %constant_dynamic-update-slice_fusion.6 = f32[8192,1024]{1,0:T(8,128)} fusion(f32[8192,1024]{1,0:T(8,128)} %constant_dynamic-update-slice_fusion.7, f32[1024,1024]{1,0:T(8,128)} %collective-permute-done.1), kind=kLoop, calls=%fused_computation.8 | loop fusion | bytes 8388608
  298.8 4.7 %constant_dynamic-update-slice_fusion.5 = f32[8192,1024]{1,0:T(8,128)} fusion(f32[8192,1024]{1,0:T(8,128)} %constant_dynamic-update-slice_fusion.6, f32[1024,1024]{1,0:T(8,128)} %collective-permute-done), kind=kLoop, calls=%fused_computation.7 | loop fusion | bytes 8388608
  303.6 4.7 %constant_dynamic-update-slice_fusion.4 = f32[8192,1024]{1,0:T(8,128)} fusion(f32[8192,1024]{1,0:T(8,128)} %constant_dynamic-update-slice_fusion.5, f32[1024,1024]{1,0:T(8,128)} %param.2), kind=kLoop, calls=%fused_computation.6 | loop fusion | bytes 8388608
  308.3 4.7 %constant_dynamic-update-slice_fusion.3 = f32[8192,1024]{1,0:T(8,128)} fusion(f32[8192,1024]{1,0:T(8,128)} %constant_dynamic-update-slice_fusion.4, f32[1024,1024]{1,0:T(8,128)} %collective-permute-done.2), kind=kLoop, calls=%fused_computation.5 | loop fusion | bytes 8388608
  313.0 4.8 %constant_dynamic-update-slice_fusion.2 = f32[8192,1024]{1,0:T(8,128)} fusion(f32[8192,1024]{1,0:T(8,128)} %constant_dynamic-update-slice_fusion.3, f32[1024,1024]{1,0:T(8,128)} %collective-permute-done.1), kind=kLoop, calls=%fused_computation.4 | loop fusion | bytes 8388608
  317.7 4.7 %constant_dynamic-update-slice_fusion.1 = f32[8192,1024]{1,0:T(8,128)} fusion(f32[8192,1024]{1,0:T(8,128)} %constant_dynamic-update-slice_fusion.2, f32[1024,1024]{1,0:T(8,128)} %collective-permute-done), kind=kLoop, calls=%fused_computation.3 | loop fusion | bytes 8388608
  322.5 0.0 copy-done
  322.5 2.2 constant_dynamic-update-slice_fusion
  324.7 0.0 all-gather.2.cloned.1.call-done
  324.7 46.7 %fusion = f32[1024,768]{1,0:T(8,128)} fusion(f32[4096,768]{1,0:T(8,128)} %all-gather.2.cloned.1.call-done, f32[8192,1024]{1,0:T(8,128)} %constant_dynamic-update-slice_fusion, s32[]{:T(128)S(6)} %select_n.14), kind=kOutput, calls=%fused_computation | convolution fusion | flops 38654705664 | bytes 32505860 | tf_op jit(solution)/shard_map/dot_general | solution.py:8
  371.4 0.0 reduce-scatter.2.cloned.1.call-update
  371.5 35.8 %reduce-scatter.2.cloned.1.call-done = f32[256,768]{1,0:T(8,128)} async-done(((f32[1024,768]{1,0:T(8,128)}), f32[256,768]{1,0:T(8,128)}) %reduce-scatter.2.cloned.1.call-update) | async-done | bytes 786448 | tf_op jit(solution)/shard_map/reduce_scatter | solution.py:26
Async XLA Ops:
  6.5 318.2 %all-gather.2.cloned.1.call-start = ((), (), s32[]{:S(2)}) async-start(), calls=%async_computation.1 | async-start | bytes 18874368 | tf_op jit(solution)/shard_map/all_gather | solution.py:18
  6.5 96.0 %collective-permute-start = (f32[1024,1024]{1,0:T(8,128)}, f32[1024,1024]{1,0:T(8,128)}, u32[]{:S(2)}, u32[]{:S(2)}) collective-permute-start(f32[1024,1024]{1,0:T(8,128)} %param.2), channel_id=1, source_target_pairs={{0,4},{4,8},{8,12},{12,0},{1,5},{5,9},{9,13},{13,1},{2,6},{6,10},{... | collective-permute-start | bytes 12582920 | tf_op jit(solution)/shard_map/ppermute | solution.py:21
  9.6 397.7 %reduce-scatter.2.cloned.1.call-start = ((), (), s32[]{:S(2)}) async-start(), calls=%async_computation.2 | async-start | bytes 3932160 | tf_op jit(solution)/shard_map/reduce_scatter | solution.py:26
  102.5 93.8 %collective-permute-start.1 = (f32[1024,1024]{1,0:T(8,128)}, f32[1024,1024]{1,0:T(8,128)}, u32[]{:S(2)}, u32[]{:S(2)}) collective-permute-start(f32[1024,1024]{1,0:T(8,128)} %collective-permute-done), channel_id=1, source_target_pairs={{0,4},{4,8},{8,12},{12,0},{1,5},{5,9},{9,13},{13,1},{2,6},{6,10},{... | collective-permute-start | bytes 12582920 | tf_op jit(solution)/shard_map/ppermute | solution.py:21
  196.3 93.0 %collective-permute-start.2 = (f32[1024,1024]{1,0:T(8,128)}, f32[1024,1024]{1,0:T(8,128)}, u32[]{:S(2)}, u32[]{:S(2)}) collective-permute-start(f32[1024,1024]{1,0:T(8,128)} %collective-permute-done.1), channel_id=1, source_target_pairs={{0,4},{4,8},{8,12},{12,0},{1,5},{5,9},{9,13},{13,1},{2,6},{6,10},{... | collective-permute-start | bytes 12582920 | tf_op jit(solution)/shard_map/ppermute | solution.py:21
  196.4 126.1 %copy-start = (f32[1024,1024]{1,0:T(8,128)S(1)}, f32[1024,1024]{1,0:T(8,128)}, u32[]{:S(2)}) copy-start(f32[1024,1024]{1,0:T(8,128)} %param.2) | copy-start | bytes 12582916
Sparse Core Ops, SparseCore 0:
  9.7 154.3 all-gather.1
  371.6 35.6 reduce-scatter.1
